TPU v7x, 32 devices: a whole 2x2x4 slice. The times are simulated.
32 devices in a mesh: loader: 32 (over z, y, x, core).
Axes of the slice: x: 2, y: 2, z: 4, core: 2. Of those that a mesh axis runs over, the one named last changes fastest.
Arguments:
- image_embed: bfloat16 [49152, 512], P('loader'), may hold values from -600 to 600
- text_embed: bfloat16 [49152, 512], P('loader'), may hold values from -600 to 600
- keep_mask: int32 [49152], P('loader'), may hold values from 0 to 1
Outputs:
- packed_pairs: bfloat16 [49152, 1024], P('loader')
- pair_scores: float32 [49152], P('loader')
All inputs are finite; a program needn't handle non-finite values.
Results may differ from a plain program's by a relative error of at most 0.002.
Values may be sent and summed in bfloat16 or wider, within the bound.
No kernel may reach another device: no remote copies, remote signals or barrier semaphores. Data moves between devices by JAX's collectives and lax.ppermute only.
A program may use at most 64 MiB of HBM per device.

v0:
```python
import jax
import jax.numpy as jnp
from jax import lax
from jax.sharding import PartitionSpec as P

epsilon = 1e-06


def from_partner(array, axis, apart):
    return lax.ppermute(array, axis, [(i, i ^ 1 << apart) for i in range(lax.axis_size(axis))])


def unit_rows(embedding):
    values = embedding.astype(jnp.float32)
    scale = lax.rsqrt(jnp.mean(values * values, axis=1, keepdims=True) + epsilon)
    return (values * scale).astype(jnp.bfloat16)


def pair_score(packed):
    halves = packed.shape[1] // 2
    left_part = packed[:, :halves].astype(jnp.float32)
    right_part = packed[:, halves:].astype(jnp.float32)
    return jnp.sum(left_part * right_part, axis=1) / halves


def compact_rows(payload, keep_mask, targets):
    row_count = payload.shape[0]
    block_rows = 512
    block_starts = jnp.arange(row_count // block_rows, dtype=jnp.int32) * block_rows

    def block_product(first_slot):
        slot_ids = first_slot + jnp.arange(block_rows, dtype=jnp.int32)
        chosen = (targets[None, :] == slot_ids[:, None]) & (keep_mask[None, :] == 1)
        return jnp.dot(
            chosen.astype(jnp.bfloat16), payload, preferred_element_type=jnp.float32
        ).astype(jnp.bfloat16)

    return lax.map(block_product, block_starts).reshape(row_count, payload.shape[1])


def moving_slots(moving, slot_low, slot_high, row_count):
    marked = moving.astype(jnp.int32)
    events = jax.ops.segment_sum(
        jnp.concatenate([marked, -marked]),
        jnp.concatenate([slot_low, slot_high]),
        num_segments=row_count + 1,
    )
    return jnp.cumsum(events)[:row_count] > 0


def shards(image_embed, text_embed, keep_mask):
    row_count = image_embed.shape[0]
    devices = lax.axis_size("loader")
    my_index = lax.axis_index("loader")
    payload = jnp.concatenate([unit_rows(image_embed), unit_rows(text_embed)], axis=1)
    local_rank = jnp.cumsum(keep_mask) - keep_mask
    kept_count = jnp.sum(keep_mask).reshape(1)
    all_counts = lax.all_gather(kept_count, "loader", axis=0, tiled=True)
    offsets = jnp.cumsum(all_counts) - all_counts
    my_offset = lax.dynamic_slice_in_dim(offsets, my_index, 1)[0]
    first_slot = my_offset % row_count
    holding = compact_rows(payload, keep_mask, (local_rank + first_slot) % row_count)
    source = jnp.arange(devices, dtype=jnp.int32)
    start_slot = offsets % row_count
    first_length = jnp.minimum(all_counts, row_count - start_slot)
    slot_low = jnp.concatenate([start_slot, jnp.zeros_like(start_slot)])
    slot_high = jnp.concatenate([start_slot + first_length, all_counts - first_length])
    anchor = jnp.concatenate([source, source])
    first_device = offsets // row_count
    target_dev = jnp.concatenate([first_device, first_device + 1])
    for bit_level in range((devices - 1).bit_length()):
        step_size = 2**bit_level
        position = anchor // step_size * step_size + target_dev % step_size
        moving = (position == my_index) & (anchor // step_size % 2 != target_dev // step_size % 2)
        leaving = moving_slots(moving, slot_low, slot_high, row_count)
        outgoing = jnp.where(leaving[:, None], holding, jnp.zeros_like(holding))
        staying = jnp.where(leaving[:, None], jnp.zeros_like(holding), holding)
        arriving = from_partner(outgoing, "loader", bit_level)
        holding = staying + arriving
    return (holding, pair_score(holding))


def solution(mesh):
    placed = (P("loader", None), P("loader", None), P("loader"))
    return jax.shard_map(
        shards,
        mesh=mesh,
        in_specs=placed,
        out_specs=(P("loader", None), P("loader")),
        check_vma=False,
    )
```

profile of v0, /device:TPU:0, one launch (start us, length us, event | category | flops | bytes accessed | tf_op | source)
XLA Modules:
  0.0 449.3 jit_solution(9391125927794815182)
XLA Ops:
  0.7 1.4 reduce_sum.36
  2.0 0.8 dynamic-update-slice
  2.8 41.9 %all-reduce.5 = s32[32]{0:T(128)S(1)} all-reduce(s32[32]{0:T(128)S(1)} %dynamic-update-slice), channel_id=1, replica_groups=mesh['loader'=32] {'loader'}, use_global_device_ids=true, to_apply=%add.5 | all-reduce | flops 32 | bytes 256
  45.4 1.3 scatter_custom_fusion.4
  46.8 0.3 reduce-window.84
  47.4 0.6 dynamic_slice.7
  48.6 1.0 reduce-window.86
  49.8 1.8 fusion.17
  51.6 1.8 fusion.15
  53.6 2.3 fusion.16
  55.9 2.1 pad_maximum_fusion
  57.9 15.4 %while.10 = (s32[]{:T(128)}, bf16[3,512,1024]{2,1,0:T(8,128)(2,1)S(1)}, s32[1536]{0:T(1024)S(1)}, s32[3]{0:T(128)S(1)}, s32[1536]{0:T(1024)S(1)}, /*index=5*/bf16[1536,1024]{1,0:T(8,128)(2,1)}, s32[]{:T(128)}) while((s32[]{:T(128)}, bf16[3,512,1024]{2,1,0:T(8,128)(2,1)S(1)}, s32[1536]{0:T(1024)S(1)}, s32[3]{0:T(128)S(1)}, ...), condition=%wide.region_22.23_spmd, body=%wide.region_21.22_spmd.sunk | while | flops 1612711936 | bytes 4216417 | solution.py:38
  57.9 0.7 dynamic_slice.9
  58.6 0.7 iota_add_fusion.2
  59.3 3.7 fusion.67
  63.1 0.7 dynamic_slice.9
  63.7 0.7 iota_add_fusion.2
  64.4 3.7 fusion.67
  68.2 0.7 dynamic_slice.9
  68.9 0.7 iota_add_fusion.2
  69.6 3.7 fusion.67
  73.3 2.6 bitcast_select_fusion
  75.9 0.2 copy-done.1
  76.1 1.3 scatter_custom_fusion.3
  77.5 0.3 reduce-window.82
  78.1 4.1 collective-permute-done
  82.1 4.6 %broadcast_select_fusion = (bf16[1536,1024]{1,0:T(8,128)(2,1)}, bf16[1536,1024]{1,0:T(8,128)(2,1)S(1)}) fusion(pred[1536]{0:T(1024)(128)(4,1)S(1)} %fusion.30, bf16[1536,1024]{1,0:T(8,128)(2,1)} %collective-permute-done, bf16[3,512,1024]{2,1,0:T(8,128)(2,1)} %copy-done.1, pred[1536]{0:T(1024)(128)(4,1)S(1)} %fusion.31), kind=kLoop, calls=%fused_computation.33 | loop fusion | flops 4718592 | bytes 12585984 | tf_op jit(solution)/shard_map/jit(_where)/select_n | solution.py:76
  86.7 2.3 collective-permute-start.1
  89.0 1.3 scatter_custom_fusion.2
  90.4 0.3 reduce-window.80
  91.0 66.7 %collective-permute-done.1 = bf16[1536,1024]{1,0:T(8,128)(2,1)} collective-permute-done((bf16[1536,1024]{1,0:T(8,128)(2,1)}, bf16[1536,1024]{1,0:T(8,128)(2,1)}, u32[]{:S(2)}, u32[]{:S(2)}) %collective-permute-start.1) | collective-permute-done | bytes 3145760 | tf_op jit(solution)/shard_map/ppermute | solution.py:10
  157.7 3.8 broadcast_select_fusion.1
  161.5 1.7 collective-permute-start.2
  163.2 1.3 scatter_custom_fusion.1
  164.6 0.3 reduce-window.78
  165.2 66.2 %collective-permute-done.2 = bf16[1536,1024]{1,0:T(8,128)(2,1)} collective-permute-done((bf16[1536,1024]{1,0:T(8,128)(2,1)}, bf16[1536,1024]{1,0:T(8,128)(2,1)}, u32[]{:S(2)}, u32[]{:S(2)}) %collective-permute-start.2) | collective-permute-done | bytes 3145760 | tf_op jit(solution)/shard_map/ppermute | solution.py:10
  231.4 7.0 %broadcast_select_fusion.2 = (bf16[1536,1024]{1,0:T(8,128)(2,1)}, bf16[1536,1024]{1,0:T(8,128)(2,1)}) fusion(pred[1536]{0:T(1024)(128)(4,1)S(1)} %fusion.28, bf16[1536,1024]{1,0:T(8,128)(2,1)} %collective-permute-done.2, bf16[1536,1024]{1,0:T(8,128)(2,1)} %collective-permute-done.1, bf16[1536,1024]{1,0:T(8,128)(2,1)S(1)} %get-tuple-element.53, ...), kind=kLoop, calls=%fused_computation.35 | loop fusion | flops 7864320 | bytes 15733248 | tf_op jit(solution)/shard_map/jit(_where)/select_n | solution.py:76
  238.3 1.5 collective-permute-start.3
  239.8 1.3 scatter_custom_fusion
  241.2 0.3 reduce-window.61
  241.8 65.5 %collective-permute-done.3 = bf16[1536,1024]{1,0:T(8,128)(2,1)S(1)} collective-permute-done((bf16[1536,1024]{1,0:T(8,128)(2,1)}, bf16[1536,1024]{1,0:T(8,128)(2,1)S(1)}, u32[]{:S(2)}, u32[]{:S(2)}) %collective-permute-start.3) | collective-permute-done | bytes 3145760 | tf_op jit(solution)/shard_map/ppermute | solution.py:10
  307.3 2.8 broadcast_select_fusion.3
  310.1 2.4 collective-permute-start.4
  312.4 133.8 %collective-permute-done.4 = bf16[1536,1024]{1,0:T(8,128)(2,1)S(1)} collective-permute-done((bf16[1536,1024]{1,0:T(8,128)(2,1)S(1)}, bf16[1536,1024]{1,0:T(8,128)(2,1)S(1)}, u32[]{:S(2)}, u32[]{:S(2)}) %collective-permute-start.4) | collective-permute-done | bytes 3145760 | tf_op jit(solution)/shard_map/ppermute | solution.py:10
  446.3 1.3 select_add_fusion
  447.6 0.5 multiply_reduce_fusion
  448.1 1.0 broadcast_multiply_fusion
  449.1 0.2 copy-done.2
  (57 shorter events, 2.6 us)
Async XLA Ops:
  0.6 52.8 %copy-start.3 = (s32[1536]{0:T(1024)S(1)}, s32[1536]{0:T(1024)}, u32[]{:S(2)}) copy-start(s32[1536]{0:T(1024)} %param.7) | copy-start | bytes 18436
  73.3 2.8 copy-start.1
  76.1 6.0 %collective-permute-start = (bf16[1536,1024]{1,0:T(8,128)(2,1)}, bf16[1536,1024]{1,0:T(8,128)(2,1)}, u32[]{:S(2)}, u32[]{:S(2)}) collective-permute-start(bf16[1536,1024]{1,0:T(8,128)(2,1)} %bitcast_select_fusion), channel_id=1, source_target_pairs={{0,1},{1,0},{2,3},{3,2},{4,5},{5,4},{6,7},{7,6},{8,9},{9,8},{10,11... | collective-permute-start | bytes 9437192 | tf_op jit(solution)/shard_map/ppermute | solution.py:10
  86.7 71.0 %collective-permute-start.1 = (bf16[1536,1024]{1,0:T(8,128)(2,1)}, bf16[1536,1024]{1,0:T(8,128)(2,1)}, u32[]{:S(2)}, u32[]{:S(2)}) collective-permute-start(bf16[1536,1024]{1,0:T(8,128)(2,1)} %get-tuple-element.52), channel_id=1, source_target_pairs={{0,2},{1,3},{2,0},{3,1},{4,6},{5,7},{6,4},{7,5},{8,10},{9,11},{10,... | collective-permute-start | bytes 9437192 | tf_op jit(solution)/shard_map/ppermute | solution.py:10
  161.5 69.9 %collective-permute-start.2 = (bf16[1536,1024]{1,0:T(8,128)(2,1)}, bf16[1536,1024]{1,0:T(8,128)(2,1)}, u32[]{:S(2)}, u32[]{:S(2)}) collective-permute-start(bf16[1536,1024]{1,0:T(8,128)(2,1)} %broadcast_select_fusion.1), channel_id=1, source_target_pairs={{0,4},{1,5},{2,6},{3,7},{4,0},{5,1},{6,2},{7,3},{8,12},{9,13},{10,... | collective-permute-start | bytes 9437192 | tf_op jit(solution)/shard_map/ppermute | solution.py:10
  238.3 68.9 %collective-permute-start.3 = (bf16[1536,1024]{1,0:T(8,128)(2,1)}, bf16[1536,1024]{1,0:T(8,128)(2,1)S(1)}, u32[]{:S(2)}, u32[]{:S(2)}) collective-permute-start(bf16[1536,1024]{1,0:T(8,128)(2,1)} %get-tuple-element.47), channel_id=1, source_target_pairs={{0,8},{1,9},{2,10},{3,11},{4,12},{5,13},{6,14},{7,15},{8,0},{9,1},... | collective-permute-start | bytes 9437192 | tf_op jit(solution)/shard_map/ppermute | solution.py:10
  307.3 139.0 %copy-start = (bf16[1536,1024]{1,0:T(8,128)(2,1)S(1)}, bf16[1536,1024]{1,0:T(8,128)(2,1)}, u32[]{:S(2)}) copy-start(bf16[1536,1024]{1,0:T(8,128)(2,1)} %get-tuple-element.48) | copy-start | bytes 9437188
  310.1 136.2 %collective-permute-start.4 = (bf16[1536,1024]{1,0:T(8,128)(2,1)S(1)}, bf16[1536,1024]{1,0:T(8,128)(2,1)S(1)}, u32[]{:S(2)}, u32[]{:S(2)}) collective-permute-start(bf16[1536,1024]{1,0:T(8,128)(2,1)S(1)} %broadcast_select_fusion.3), channel_id=1, source_target_pairs={{0,16},{1,17},{2,18},{3,19},{4,20},{5,21},{6,22},{7,23},{8,24},{9,... | collective-permute-start | bytes 9437192 | tf_op jit(solution)/shard_map/ppermute | solution.py:10
  447.6 1.7 copy-start.2
where the time goes:
time: 450 us; the launch traced here: 449 us
  waiting for transfers between devices  336 us (75%)
  other arithmetic  45.4 us (10%)
  blocking collectives  41.9 us (9%)
  matrix products  11.2 us (2%)
  starting transfers between devices  7.9 us (2%)
  local copies, waits for them, and re-layouts  5 us (1%)
    ppermute x5, waiting for transfers between devices, from_partner(): lax.ppermute(array, axis, [(i, i ^ 1 << apart) for i in range(lax.axis_si...  336 us
    unnamed x1, blocking collectives  41.9 us
    select_n x5, other arithmetic, shards(): outgoing = jnp.where(leaving[:, None], holding, jnp.zeros_like(holding))  20.7 us
    dot_general x3, matrix products, block_product(): jnp.dot(chosen.astype(jnp.bfloat16), payload, preferred_element_type=jnp....  11.2 us
  transfers between devices with their start and end apart: 5, of which 5 were waited for; matrix products, arithmetic and copies ran while one was open for 2% of the time, Pallas kernels for 0%

commit v1 on v0

v1 whole, which is shorter than its diff:
```python
import functools

import jax
import jax.numpy as jnp
from jax import lax
from jax.experimental import pallas as pl
from jax.experimental.pallas import tpu as pltpu
from jax.sharding import PartitionSpec as P

epsilon = 1e-06
TILE = 16
BLOCK = 256
WINDOWS = ((768, 704), (1024, 1024, 256))

SMEM = pl.BlockSpec(memory_space=pltpu.SMEM)
VMEM = pl.BlockSpec(memory_space=pltpu.VMEM)


def group_of(devices):
    return 2 ** (devices.bit_length() // 2)


def before(counts_ref, index):
    return lax.fori_loop(0, index, lambda s, total: total + counts_ref[s], jnp.int32(0))


def dealt(rank, member, group):
    turn = group * TILE
    return rank // turn * TILE + jnp.clip(rank % turn - member * TILE, 0, TILE)


def pack_kernel(group, counts_ref, sums_ref, mask_ref, x_ref, *rest):
    outs, packed, ahead = rest[:group], rest[group], rest[group + 1]
    rows, width = x_ref.shape
    blocks = rows // BLOCK
    me = lax.axis_index("loader")
    member = me % group
    packed[...] = jnp.zeros_like(packed)
    r = lax.broadcasted_iota(jnp.int32, (BLOCK, BLOCK), 0)
    c = lax.broadcasted_iota(jnp.int32, (BLOCK, BLOCK), 1)
    triangle = (r < c).astype(jnp.float32).astype(jnp.bfloat16)
    marks = mask_ref[...].astype(jnp.float32).astype(jnp.bfloat16)
    ahead[...] = jnp.dot(marks, triangle, preferred_element_type=jnp.float32).astype(jnp.int32)

    def step(b, base):
        values = x_ref[pl.ds(pl.multiple_of(b * BLOCK, BLOCK), BLOCK), :].astype(jnp.float32)
        scale = lax.rsqrt(jnp.sum(values * values, axis=1, keepdims=True) / width + epsilon)
        unit = (values * scale).astype(jnp.bfloat16)
        kept = mask_ref[pl.ds(b, 1), :] == 1
        into = base % BLOCK
        slot = jnp.where(kept, ahead[pl.ds(b, 1), :] + into, -1)

        def put(first, block):
            chosen = (slot - first == r).astype(jnp.float32).astype(jnp.bfloat16)
            part = jnp.dot(chosen, unit, preferred_element_type=jnp.float32).astype(jnp.bfloat16)
            for e in range(BLOCK // TILE):
                at = block * (BLOCK // TILE // group) + e // group
                where = pl.ds(pl.multiple_of(at * TILE, TILE), TILE)
                packed[e % group, where, :] += part[e * TILE : (e + 1) * TILE]

        count = sums_ref[b]

        @pl.when(count > 0)
        def _():
            put(0, base // BLOCK)

        @pl.when(into + count > BLOCK)
        def _():
            put(BLOCK, (base // BLOCK + 1) % blocks)

        return (base + count) % rows

    lax.fori_loop(0, blocks, step, before(counts_ref, me) % rows)
    for k in range(group):
        outs[k][...] = packed[jnp.bitwise_xor(member, k)]


def copy_rows(low, high, source, source_tile, target, target_tile):
    width = target.shape[-1]

    def tile(t, _):
        row = t * TILE + lax.broadcasted_iota(jnp.int32, (TILE, width), 0)
        inside = (row >= low) & (row < high)
        at = pl.ds(pl.multiple_of(target_tile(t) * TILE, TILE), TILE)
        value = source[pl.ds(pl.multiple_of(source_tile(t) * TILE, TILE), TILE), :]
        target[at, :] = jnp.where(inside, value, target[at, :])
        return 0

    lax.fori_loop(low // TILE, jnp.where(high > low, (high + TILE - 1) // TILE, low // TILE), tile, 0)


def window_start(counts_ref, plane, group):
    return before(counts_ref, plane * group) // (group * TILE)


def window_kernel(group, counts_ref, *rest):
    parts, window = rest[:group], rest[group]
    me = lax.axis_index("loader")
    member, plane = me % group, me // group
    tiles = parts[0].shape[0] // TILE
    start = window_start(counts_ref, plane, group)
    for k in range(group):
        source = plane * group + jnp.bitwise_xor(member, k)
        ranks = before(counts_ref, source)
        low = dealt(ranks, member, group)
        high = dealt(ranks + counts_ref[source], member, group)
        high = jnp.minimum(high, start * TILE + window.shape[0])
        copy_rows(low, high, parts[k], lambda t: t % tiles, window, lambda t: t - start)


def place_window(counts_ref, apart, group, rows, window, target):
    me = lax.axis_index("loader")
    member, plane = me % group, me // group
    origin = plane + apart
    planes = counts_ref.shape[0] // group
    bounded = jnp.minimum(origin, planes - 1)
    ranks = before(counts_ref, bounded * group)
    low = jnp.maximum(dealt(ranks, member, group), rows * plane)
    high = dealt(before(counts_ref, (bounded + 1) * group), member, group)
    high = jnp.where(origin < planes, jnp.minimum(high, rows * (plane + 1)), low)
    start = ranks // (group * TILE)
    first = rows // TILE * plane
    copy_rows(low, high, window, lambda t: t - start, target, lambda t: t - first)


def place_own(counts_ref, group, rows, parts, target):
    me = lax.axis_index("loader")
    member, plane = me % group, me // group
    tiles = parts[0].shape[0] // TILE
    first = rows // TILE * plane
    target[...] = jnp.zeros_like(target)
    for k in range(group):
        source = plane * group + jnp.bitwise_xor(member, k)
        ranks = before(counts_ref, source)
        low = jnp.maximum(dealt(ranks, member, group), rows * plane)
        high = jnp.minimum(dealt(ranks + counts_ref[source], member, group), rows * (plane + 1))
        copy_rows(low, high, parts[k], lambda t: t % tiles, target, lambda t: t - first)


def assemble_kernel(group, hops, counts_ref, *rest):
    parts, windows = rest[:group], rest[group : group + hops]
    outs, target = rest[group + hops : -1], rest[-1]
    rows = target.shape[0]
    place_own(counts_ref, group, rows, parts, target)
    for k in range(hops):
        place_window(counts_ref, k + 1, group, rows, windows[k], target)
    member = lax.axis_index("loader") % group
    share = rows // group
    for k in range(group):
        chunk = jnp.bitwise_xor(member, k) * share
        outs[k][...] = target[pl.ds(pl.multiple_of(chunk, TILE), share), :]


def own_kernel(group, counts_ref, *rest):
    place_own(counts_ref, group, rest[group].shape[0], rest[:group], rest[group])


def place_kernel(group, counts_ref, apart_ref, window, held, target):
    target[...] = held[...]
    place_window(counts_ref, apart_ref[0], group, target.shape[0], window, target)


def finish_kernel(group, *rest):
    left, right = rest[:group], rest[group : 2 * group]
    packed, scores = rest[2 * group :]
    width = left[0].shape[1]
    member = lax.axis_index("loader") % group
    tiles = left[0].shape[0] // TILE
    for k in range(group):
        owner = jnp.bitwise_xor(member, k)
        for t in range(tiles):
            at = pl.ds(pl.multiple_of((t * group + owner) * TILE, TILE), TILE)
            packed[at, :width] = left[k][t * TILE : (t + 1) * TILE, :]
            packed[at, width:] = right[k][t * TILE : (t + 1) * TILE, :]
    lanes = scores.shape[1]
    r = lax.broadcasted_iota(jnp.int32, (lanes, lanes), 0)
    c = lax.broadcasted_iota(jnp.int32, (lanes, lanes), 1)
    for s in range(scores.shape[0]):
        at = pl.ds(s * lanes, lanes)
        products = lax.dot_general(
            packed[at, :width], packed[at, width:], (((1,), (1,)), ((), ())), preferred_element_type=jnp.float32
        )
        own = jnp.where(r == c, products, 0.0)
        scores[s : s + 1, :] = jnp.sum(own, axis=0, keepdims=True) / width


def window_class_kernel(group, classes, counts_ref, class_ref):
    devices = counts_ref.shape[0]
    planes = devices // group
    turn = group * TILE
    edges = [jnp.int32(0)]
    for p in range(planes):
        edges.append(
            lax.fori_loop(p * group, (p + 1) * group, lambda s, total: total + counts_ref[s], edges[-1])
        )
    needed = []
    rows = classes[-1]
    for hop in range(1, planes):
        most = jnp.int32(0)
        for p in range(hop, planes):
            end = jnp.minimum(edges[p + 1], group * rows * (p - hop + 1))
            length = ((end + turn - 1) // turn - edges[p] // turn) * TILE
            most = jnp.maximum(most, jnp.where(end > edges[p], length, 0))
        needed.append(most)
    chosen = jnp.int32(len(classes) - 1)
    for index in reversed(range(len(classes) - 1)):
        fits = jnp.bool_(True)
        for hop in range(planes - 1):
            room = classes[index][hop] if hop < len(classes[index]) else 0
            fits = fits & (needed[hop] <= room)
        chosen = jnp.where(fits, jnp.int32(index), chosen)
    class_ref[0] = chosen


def all_counts_of(count, devices):
    me = lax.axis_index("loader")
    known = jnp.where(jnp.arange(devices, dtype=jnp.int32) == me, count, 0)
    for level in range((devices - 1).bit_length()):
        known = known + lax.ppermute(known, "loader", [(i, i ^ 1 << level) for i in range(devices)])
    return known


def exchange(parts, devices):
    received = [parts[0]]
    for k in range(1, len(parts)):
        received.append(lax.ppermute(parts[k], "loader", [(i, i ^ k) for i in range(devices)]))
    return received


def shards(image_embed, text_embed, keep_mask):
    rows, width = image_embed.shape
    devices = lax.axis_size("loader")
    group = group_of(devices)
    planes = devices // group
    share = rows // group
    dtype = image_embed.dtype
    part = jax.ShapeDtypeStruct((share, width), dtype)
    whole = jax.ShapeDtypeStruct((rows, width), dtype)

    marks = keep_mask.reshape(rows // BLOCK, BLOCK)
    sums = jnp.sum(marks, axis=1)
    counts = all_counts_of(jnp.sum(sums), devices)

    def pack(embed):
        return pl.pallas_call(
            functools.partial(pack_kernel, group),
            out_shape=[part] * group,
            in_specs=[SMEM, SMEM, VMEM, VMEM],
            out_specs=[VMEM] * group,
            scratch_shapes=[
                pltpu.VMEM((group, share, width), dtype),
                pltpu.VMEM(marks.shape, jnp.int32),
            ],
            name="pack",
        )(counts, sums, marks, embed)

    def window_of(parts, length):
        return pl.pallas_call(
            functools.partial(window_kernel, group),
            out_shape=jax.ShapeDtypeStruct((length, width), dtype),
            in_specs=[SMEM] + [VMEM] * group,
            out_specs=VMEM,
            name="window",
        )(counts, *parts)

    def assemble(parts, windows):
        return pl.pallas_call(
            functools.partial(assemble_kernel, group, len(windows)),
            out_shape=[part] * group,
            in_specs=[SMEM] + [VMEM] * (group + len(windows)),
            out_specs=[VMEM] * group,
            scratch_shapes=[pltpu.VMEM((rows, width), dtype)],
            name="assemble",
        )(counts, *parts, *windows)

    def down(window):
        return lax.ppermute(window, "loader", [(i, i - group) for i in range(group, devices)])

    def finish(left, right):
        packed, scores = pl.pallas_call(
            functools.partial(finish_kernel, group),
            out_shape=[
                jax.ShapeDtypeStruct((rows, 2 * width), dtype),
                jax.ShapeDtypeStruct((rows // 128, 128), jnp.float32),
            ],
            in_specs=[VMEM] * (2 * group),
            out_specs=[VMEM] * 2,
            name="finish",
        )(*left, *right)
        return packed, scores.reshape(rows)

    def fixed(lengths):
        def run(received, other):
            halves = [received, exchange(other, devices)]
            done = []
            for parts in halves:
                window = window_of(parts, lengths[0])
                windows = []
                for length in lengths:
                    window = down(window[:length])
                    windows.append(window)
                done.append(exchange(assemble(parts, windows), devices))
            return finish(*done)

        return run

    def general(received, other):
        halves = [received, exchange(other, devices)]
        member = lax.axis_index("loader") % group
        done = []
        for parts in halves:
            window = window_of(parts, rows + TILE)
            held = pl.pallas_call(
                functools.partial(own_kernel, group),
                out_shape=whole,
                in_specs=[SMEM] + [VMEM] * group,
                out_specs=VMEM,
                name="own",
            )(counts, *parts)

            def hop(k, state):
                window, held = state
                window = down(window)
                held = pl.pallas_call(
                    functools.partial(place_kernel, group),
                    out_shape=whole,
                    in_specs=[SMEM, SMEM, VMEM, VMEM],
                    out_specs=VMEM,
                    name="place",
                )(counts, k.reshape(1), window, held)
                return window, held

            _, held = lax.fori_loop(1, planes, hop, (window, held))
            chunks = held.reshape(group, share, width)
            parts = [lax.dynamic_index_in_dim(chunks, member ^ k, 0, keepdims=False) for k in range(group)]
            done.append(exchange(parts, devices))
        return finish(*done)

    lengths = [w for w in WINDOWS if w[0] <= rows and len(w) < planes]
    chosen = pl.pallas_call(
        functools.partial(window_class_kernel, group, tuple(lengths) + (rows,)),
        out_shape=jax.ShapeDtypeStruct((1,), jnp.int32),
        in_specs=[SMEM],
        out_specs=SMEM,
        name="choose",
    )(counts)
    received = exchange(pack(image_embed), devices)
    other = pack(text_embed)
    branches = [fixed(w) for w in lengths] + [general]
    return lax.switch(chosen[0], branches, received, other)


def solution(mesh):
    placed = (P("loader", None), P("loader", None), P("loader"))
    return jax.shard_map(
        shards,
        mesh=mesh,
        in_specs=placed,
        out_specs=(P("loader", None), P("loader")),
        check_vma=False,
    )
```

time: 450 us -> 213 us (0.47)
  waiting for transfers between devices: 336 us -> 120 us
  starting transfers between devices: 7.9 us -> 52.1 us
  blocking collectives: 41.9 us -> 0 us
  other arithmetic: 45.4 us -> 3.94 us
  Pallas kernels: 0 us -> 31.3 us
  matrix products: 11.2 us -> 0 us
    ppermute x5 -> x39, waiting for transfers between devices: 336 us -> 120 us  [the longest x6 80.4 us: down(): lax.ppermute(window, 'loader', [(i, i - group) for i in range(group, devi...]
    ppermute x5 -> x39, starting transfers between devices: 7.9 us -> 52.1 us  [the longest x28 33.7 us: exchange(): lax.ppermute(parts[k], 'loader', [(i, i ^ k) for i in range(devices)])]
    unnamed x1 -> x0, blocking collectives: 41.9 us -> none
    pallas_call x0 -> x8, Pallas kernels: none -> 31.3 us  [the longest x2 10.6 us: assemble(): pl.pallas_call(functools.partial(assemble_kernel, group, len(windows)), o...]
    select_n x6 -> x1, other arithmetic: 20.8 us -> 0.65 us  [all_counts_of(): known = jnp.where(jnp.arange(devices, dtype=jnp.int32) == me, count, 0)]
    dot_general x3 -> x0, matrix products: 11.2 us -> none  [block_product(): jnp.dot(chosen.astype(jnp.bfloat16), payload, preferred_element_type=jnp....]
    scatter-add x5 -> x0, other arithmetic: 6.71 us -> none  [moving_slots(): jax.ops.segment_sum(jnp.concatenate([marked, -marked]), jnp.concatenate([...]
  transfers between devices with their start and end apart: 5 -> 39, of which waited for: 5 -> 19; matrix products, arithmetic and copies ran while one was open for 2% -> 1% of each run, Pallas kernels for 0% -> 11%
where the time goes in v1:
time: 213 us
  waiting for transfers between devices  120 us (56%)
  starting transfers between devices  52.1 us (24%)
  Pallas kernels  31.3 us (15%)
  other arithmetic  3.94 us (2%)
  local copies, waits for them, and re-layouts  3.76 us (2%)
    ppermute x6, waiting for transfers between devices, down(): lax.ppermute(window, 'loader', [(i, i - group) for i in range(group, devi...  80.4 us
    ppermute x28, waiting for transfers between devices, exchange(): lax.ppermute(parts[k], 'loader', [(i, i ^ k) for i in range(devices)])  34.1 us
    ppermute x28, starting transfers between devices, exchange(): lax.ppermute(parts[k], 'loader', [(i, i ^ k) for i in range(devices)])  33.7 us
    ppermute x5, starting transfers between devices, all_counts_of(): lax.ppermute(known, 'loader', [(i, i ^ 1 << level) for i in range(devices)])  10.7 us
    pallas_call x2, Pallas kernels, assemble(): pl.pallas_call(functools.partial(assemble_kernel, group, len(windows)), o...  10.6 us
    pallas_call x2, Pallas kernels, pack(): pl.pallas_call(functools.partial(pack_kernel, group), out_shape=[part] *...  10 us
    ppermute x6, starting transfers between devices, down(): lax.ppermute(window, 'loader', [(i, i - group) for i in range(group, devi...  7.69 us
    ppermute x5, waiting for transfers between devices, all_counts_of(): lax.ppermute(known, 'loader', [(i, i ^ 1 << level) for i in range(devices)])  5.65 us
  transfers between devices with their start and end apart: 39, of which 19 were waited for; matrix products, arithmetic and copies ran while one was open for 1% of the time, Pallas kernels for 11%

profile of v1, /device:TPU:0, one launch (start us, length us, event | category | flops | bytes accessed | tf_op | source)
XLA Modules:
  0.0 212.8 jit_solution(6441647955424773666)
XLA Ops:
  0.6 1.3 reduce_sum.18
  4.7 2.9 %collective-permute-start.76 = (s32[32]{0:T(128)S(1)}, s32[32]{0:T(128)S(1)}, u32[]{:S(2)}, u32[]{:S(2)}) collective-permute-start(s32[32]{0:T(128)S(1)} %fusion), channel_id=1, source_target_pairs={{0,2},{1,3},{2,0},{3,1},{4,6},{5,7},{6,4},{7,5},{8,10},{9,11},{10,... | collective-permute-start | bytes 392 | tf_op jit(solution)/shard_map/ppermute | solution.py:219
  7.5 1.5 collective-permute-done.76
  9.7 2.1 collective-permute-start.77
  11.9 1.5 collective-permute-done.77
  13.4 2.1 collective-permute-start.78
  15.5 1.5 collective-permute-done.78
  17.0 3.0 %collective-permute-start.79 = (s32[32]{0:T(128)S(1)}, s32[32]{0:T(128)S(1)}, u32[]{:S(2)}, u32[]{:S(2)}) collective-permute-start(s32[32]{0:T(128)S(1)} %add.87), channel_id=1, source_target_pairs={{0,16},{1,17},{2,18},{3,19},{4,20},{5,21},{6,22},{7,23},{8,24},{9,... | collective-permute-start | bytes 392 | tf_op jit(solution)/shard_map/ppermute | solution.py:219
  21.6 5.0 %pack.2 = (bf16[192,512]{1,0:T(8,128)(2,1)S(1)}, bf16[192,512]{1,0:T(8,128)(2,1)}, bf16[192,512]{1,0:T(8,128)(2,1)}, bf16[192,512]{1,0:T(8,128)(2,1)}, bf16[192,...) custom-call(s32[32]{0:T(128)S(1)} %add.88.counts_ref, ...), custom_call_target="tpu_custom_call" | custom-call | tf_op jit(solution)/shard_map/pack/pallas_call | solution.py:245
  26.6 2.8 %collective-permute-start.81 = (bf16[192,512]{1,0:T(8,128)(2,1)}, bf16[192,512]{1,0:T(8,128)(2,1)S(1)}, u32[]{:S(2)}, u32[]{:S(2)}) collective-permute-start(bf16[192,512]{1,0:T(8,128)(2,1)} %get-tuple-element.359), channel_id=1, source_target_pairs={{0,2},{1,3},{2,0},{3,1},{4,6},{5,7},{6,4},{7,5},{8,10},{9,11},{10,... | collective-permute-start | bytes 589832 | tf_op jit(solution)/shard_map/ppermute | solution.py:226
  29.5 1.3 collective-permute-start.83
  30.9 2.2 %collective-permute-start.85 = (bf16[192,512]{1,0:T(8,128)(2,1)}, bf16[192,512]{1,0:T(8,128)(2,1)S(1)}, u32[]{:S(2)}, u32[]{:S(2)}) collective-permute-start(bf16[192,512]{1,0:T(8,128)(2,1)} %get-tuple-element.363), channel_id=1, source_target_pairs={{0,6},{1,7},{2,4},{3,5},{4,2},{5,3},{6,0},{7,1},{8,14},{9,15},{10,... | collective-permute-start | bytes 589832 | tf_op jit(solution)/shard_map/ppermute | solution.py:226
  33.2 2.2 %collective-permute-done.81 = bf16[192,512]{1,0:T(8,128)(2,1)S(1)} collective-permute-done((bf16[192,512]{1,0:T(8,128)(2,1)}, bf16[192,512]{1,0:T(8,128)(2,1)S(1)}, u32[]{:S(2)}, u32[]{:S(2)}) %collective-permute-start.81) | collective-permute-done | bytes 196640 | tf_op jit(solution)/shard_map/ppermute | solution.py:226
  35.3 1.0 collective-permute-start.86
  36.4 1.3 choose.1
  37.7 5.0 %pack.3 = (bf16[192,512]{1,0:T(8,128)(2,1)S(1)}, bf16[192,512]{1,0:T(8,128)(2,1)}, bf16[192,512]{1,0:T(8,128)(2,1)}, bf16[192,512]{1,0:T(8,128)(2,1)}, bf16[192,...) custom-call(s32[32]{0:T(128)S(1)} %add.88.counts_ref, ...), custom_call_target="tpu_custom_call" | custom-call | tf_op jit(solution)/shard_map/pack/pallas_call | solution.py:245
  43.4 5.0 %collective-permute-done.84 = bf16[192,512]{1,0:T(8,128)(2,1)S(1)} collective-permute-done((bf16[192,512]{1,0:T(8,128)(2,1)}, bf16[192,512]{1,0:T(8,128)(2,1)S(1)}, u32[]{:S(2)}, u32[]{:S(2)}) %collective-permute-start.84) | collective-permute-done | bytes 196640 | tf_op jit(solution)/shard_map/ppermute | solution.py:226
  48.4 164.4 %conditional.1 = (bf16[1536,1024]{1,0:T(8,128)(2,1)}, f32[1536]{0:T(1024)}) conditional(s32[]{:T(128)} %bitcast.23, (s32[32]{0:T(128)S(1)}, bf16[192,512]{1,0:T(8,128)(2,1)S(1)}, bf16[192,512]{1,0:T(8,128)(2,1)S(1)}, bf16[192,512]{1,0:T(8,128)(2,1)S(1)}, bf16[192,512]{1,0:T(8,128)(2,1)S(1)}, ...), branch_computations={%region_2.3_spmd, %region_3.4_spmd, %region_4.9_spmd} | conditional | flops 48 | bytes 75040952 | solution.py:350
  49.1 1.9 collective-permute-start.36
  51.0 1.0 collective-permute-start.38
  52.6 2.2 %collective-permute-start.40 = (bf16[192,512]{1,0:T(8,128)(2,1)}, bf16[192,512]{1,0:T(8,128)(2,1)S(1)}, u32[]{:S(2)}, u32[]{:S(2)}) collective-permute-start(bf16[192,512]{1,0:T(8,128)(2,1)} %get-tuple-element.296), channel_id=1, source_target_pairs={{0,6},{1,7},{2,4},{3,5},{4,2},{5,3},{6,0},{7,1},{8,14},{9,15},{10,... | collective-permute-start | bytes 589832 | tf_op jit(solution)/shard_map/cond/branch_1_fun/ppermute | solution.py:226
  54.8 2.3 %collective-permute-done.36.rest_2_ = bf16[192,512]{1,0:T(8,128)(2,1)S(1)} collective-permute-done((bf16[192,512]{1,0:T(8,128)(2,1)}, bf16[192,512]{1,0:T(8,128)(2,1)S(1)}, u32[]{:S(2)}, u32[]{:S(2)}) %collective-permute-start.36) | collective-permute-done | bytes 196640 | tf_op jit(solution)/shard_map/cond/branch_1_fun/ppermute | solution.py:226
  57.2 2.4 %window.8 = bf16[1024,512]{1,0:T(8,128)(2,1)} custom-call(s32[32]{0:T(128)S(1)} %get-tuple-element.273.counts_ref, bf16[192,512]{1,0:T(8,128)(2,1)S(1)} %get-tuple-element.274.rest_0_, bf16[192,512]{1,0:T(8,128)(2,1)S(1)} %get-tuple-element.275.rest_1_, bf16[192,512]{1,0:T(8,128)(2,1)S(1)} %get-tuple-element.276.rest_2_, ...), custom_call_target="tpu_custom_call" | custom-call | tf_op jit(solution)/shard_map/cond/branch_1_fun/window/pallas_call | solution.py:258
  59.6 1.3 collective-permute-done.37.rest_3_
  60.8 1.3 collective-permute-start.25
  62.1 7.9 %collective-permute-done.39.rest_5_ = bf16[192,512]{1,0:T(8,128)(2,1)S(1)} collective-permute-done((bf16[192,512]{1,0:T(8,128)(2,1)}, bf16[192,512]{1,0:T(8,128)(2,1)S(1)}, u32[]{:S(2)}, u32[]{:S(2)}) %collective-permute-start.39) | collective-permute-done | bytes 196640 | tf_op jit(solution)/shard_map/cond/branch_1_fun/ppermute | solution.py:226
  70.9 3.2 %window.9 = bf16[1024,512]{1,0:T(8,128)(2,1)} custom-call(s32[32]{0:T(128)S(1)} %get-tuple-element.273.counts_ref, bf16[192,512]{1,0:T(8,128)(2,1)S(1)} %get-tuple-element.290.rest_0_, bf16[192,512]{1,0:T(8,128)(2,1)} %copy-done.9, bf16[192,512]{1,0:T(8,128)(2,1)} %copy-done.10, bf16[192,512]{1,0:T(8,128)(2,1)} %copy-done.11, bf16[192,512]{1,0:T(8,128)(2,1)} %copy-done.12, ...), custom_call_target="tpu_custom_call" | custom-call | tf_op jit(solution)/shard_map/cond/branch_1_fun/window/pallas_call | solution.py:258
  74.2 1.3 collective-permute-start.42
  75.5 13.4 %collective-permute-done.25.rest_8_ = bf16[1024,512]{1,0:T(8,128)(2,1)} collective-permute-done((bf16[1024,512]{1,0:T(8,128)(2,1)}, bf16[1024,512]{1,0:T(8,128)(2,1)}, u32[]{:S(2)}, u32[]{:S(2)}) %collective-permute-start.25) | collective-permute-done | bytes 1048608 | tf_op jit(solution)/shard_map/cond/branch_1_fun/ppermute | solution.py:277
  88.9 1.3 collective-permute-start.26
  90.2 21.1 %collective-permute-done.42.rest_8_ = bf16[1024,512]{1,0:T(8,128)(2,1)S(1)} collective-permute-done((bf16[1024,512]{1,0:T(8,128)(2,1)}, bf16[1024,512]{1,0:T(8,128)(2,1)S(1)}, u32[]{:S(2)}, u32[]{:S(2)}) %collective-permute-start.42) | collective-permute-done | bytes 1048608 | tf_op jit(solution)/shard_map/cond/branch_1_fun/ppermute | solution.py:277
  111.3 1.3 collective-permute-start.43
  112.6 21.2 %collective-permute-done.26.rest_9_ = bf16[1024,512]{1,0:T(8,128)(2,1)S(1)} collective-permute-done((bf16[1024,512]{1,0:T(8,128)(2,1)}, bf16[1024,512]{1,0:T(8,128)(2,1)S(1)}, u32[]{:S(2)}, u32[]{:S(2)}) %collective-permute-start.26) | collective-permute-done | bytes 1048608 | tf_op jit(solution)/shard_map/cond/branch_1_fun/ppermute | solution.py:277
  133.8 1.3 collective-permute-start.27
  135.1 21.1 %collective-permute-done.43.rest_9_ = bf16[1024,512]{1,0:T(8,128)(2,1)S(1)} collective-permute-done((bf16[1024,512]{1,0:T(8,128)(2,1)S(1)}, bf16[1024,512]{1,0:T(8,128)(2,1)S(1)}, u32[]{:S(2)}, u32[]{:S(2)}) %collective-permute-start.43) | collective-permute-done | bytes 1048608 | tf_op jit(solution)/shard_map/cond/branch_1_fun/ppermute | solution.py:277
  157.0 1.3 collective-permute-start.44
  158.3 3.6 %collective-permute-done.27.rest_10_ = bf16[256,512]{1,0:T(8,128)(2,1)S(1)} collective-permute-done((bf16[256,512]{1,0:T(8,128)(2,1)S(1)}, bf16[256,512]{1,0:T(8,128)(2,1)S(1)}, u32[]{:S(2)}, u32[]{:S(2)}) %collective-permute-start.27) | collective-permute-done | bytes 262176 | tf_op jit(solution)/shard_map/cond/branch_1_fun/ppermute | solution.py:277
  162.5 5.0 %assemble.6 = (bf16[192,512]{1,0:T(8,128)(2,1)}, bf16[192,512]{1,0:T(8,128)(2,1)}, bf16[192,512]{1,0:T(8,128)(2,1)}, bf16[192,512]{1,0:T(8,128)(2,1)}, bf16[192,...) custom-call(s32[32]{0:T(128)S(1)} %get-tuple-element.273.counts_ref, ...), custom_call_target="tpu_custom_call" | custom-call | tf_op jit(solution)/shard_map/cond/branch_1_fun/assemble/pallas_call | solution.py:267
  170.2 1.1 collective-permute-start.32
  171.3 5.6 %assemble.7 = (bf16[192,512]{1,0:T(8,128)(2,1)}, bf16[192,512]{1,0:T(8,128)(2,1)}, bf16[192,512]{1,0:T(8,128)(2,1)}, bf16[192,512]{1,0:T(8,128)(2,1)}, bf16[192,...) custom-call(s32[32]{0:T(128)S(1)} %get-tuple-element.273.counts_ref, ...), custom_call_target="tpu_custom_call" | custom-call | tf_op jit(solution)/shard_map/cond/branch_1_fun/assemble/pallas_call | solution.py:267
  177.9 1.8 collective-permute-start.34
  181.0 8.8 %collective-permute-start.47 = (bf16[192,512]{1,0:T(8,128)(2,1)}, bf16[192,512]{1,0:T(8,128)(2,1)S(1)}, u32[]{:S(2)}, u32[]{:S(2)}) collective-permute-start(bf16[192,512]{1,0:T(8,128)(2,1)} %get-tuple-element.301), channel_id=1, source_target_pairs={{0,3},{1,2},{2,1},{3,0},{4,7},{5,6},{6,5},{7,4},{8,11},{9,10},{10,... | collective-permute-start | bytes 589832 | tf_op jit(solution)/shard_map/cond/branch_1_fun/ppermute | solution.py:226
  191.0 1.2 collective-permute-start.50
  192.2 1.3 collective-permute-done.46.rest_10_
  194.1 2.1 collective-permute-done.47.rest_11_
  196.2 2.0 collective-permute-done.48.rest_12_
  198.3 9.9 %collective-permute-done.49.rest_13_ = bf16[192,512]{1,0:T(8,128)(2,1)S(1)} collective-permute-done((bf16[192,512]{1,0:T(8,128)(2,1)}, bf16[192,512]{1,0:T(8,128)(2,1)S(1)}, u32[]{:S(2)}, u32[]{:S(2)}) %collective-permute-start.49) | collective-permute-done | bytes 196640 | tf_op jit(solution)/shard_map/cond/branch_1_fun/ppermute | solution.py:226
  209.0 3.8 %finish.4 = (bf16[1536,1024]{1,0:T(8,128)(2,1)}, f32[12,128]{1,0:T(8,128)}) custom-call(bf16[192,512]{1,0:T(8,128)(2,1)} %get-tuple-element.282.rest_0_, bf16[192,512]{1,0:T(8,128)(2,1)} %copy-done.29, bf16[192,512]{1,0:T(8,128)(2,1)} %copy-done.31, bf16[192,512]{1,0:T(8,128)(2,1)} %copy-done.33, bf16[192,512]{1,0:T(8,128)(2,1)} %copy-done.35, ...), custom_call_target="tpu_custom_call" | custom-call | tf_op jit(solution)/shard_map/cond/branch_1_fun/finish/pallas_call | solution.py:280
  (108 shorter events, 16.3 us)
Async XLA Ops:
  2.6 1.4 collective-permute-start.75
  4.7 4.4 %collective-permute-start.76 = (s32[32]{0:T(128)S(1)}, s32[32]{0:T(128)S(1)}, u32[]{:S(2)}, u32[]{:S(2)}) collective-permute-start(s32[32]{0:T(128)S(1)} %fusion), channel_id=1, source_target_pairs={{0,2},{1,3},{2,0},{3,1},{4,6},{5,7},{6,4},{7,5},{8,10},{9,11},{10,... | collective-permute-start | bytes 392 | tf_op jit(solution)/shard_map/ppermute | solution.py:219
  9.7 3.7 %collective-permute-start.77 = (s32[32]{0:T(128)S(1)}, s32[32]{0:T(128)S(1)}, u32[]{:S(2)}, u32[]{:S(2)}) collective-permute-start(s32[32]{0:T(128)S(1)} %fusion.1), channel_id=1, source_target_pairs={{0,4},{1,5},{2,6},{3,7},{4,0},{5,1},{6,2},{7,3},{8,12},{9,13},{10,... | collective-permute-start | bytes 392 | tf_op jit(solution)/shard_map/ppermute | solution.py:219
  13.4 3.6 %collective-permute-start.78 = (s32[32]{0:T(128)S(1)}, s32[32]{0:T(128)S(1)}, u32[]{:S(2)}, u32[]{:S(2)}) collective-permute-start(s32[32]{0:T(128)S(1)} %add.86), channel_id=1, source_target_pairs={{0,8},{1,9},{2,10},{3,11},{4,12},{5,13},{6,14},{7,15},{8,0},{9,1},... | collective-permute-start | bytes 392 | tf_op jit(solution)/shard_map/ppermute | solution.py:219
  17.0 4.6 %collective-permute-start.79 = (s32[32]{0:T(128)S(1)}, s32[32]{0:T(128)S(1)}, u32[]{:S(2)}, u32[]{:S(2)}) collective-permute-start(s32[32]{0:T(128)S(1)} %add.87), channel_id=1, source_target_pairs={{0,16},{1,17},{2,18},{3,19},{4,20},{5,21},{6,22},{7,23},{8,24},{9,... | collective-permute-start | bytes 392 | tf_op jit(solution)/shard_map/ppermute | solution.py:219
  26.6 4.3 %collective-permute-start.80 = (bf16[192,512]{1,0:T(8,128)(2,1)}, bf16[192,512]{1,0:T(8,128)(2,1)S(1)}, u32[]{:S(2)}, u32[]{:S(2)}) collective-permute-start(bf16[192,512]{1,0:T(8,128)(2,1)} %get-tuple-element.358), channel_id=1, source_target_pairs={{0,1},{1,0},{2,3},{3,2},{4,5},{5,4},{6,7},{7,6},{8,9},{9,8},{10,11... | collective-permute-start | bytes 589832 | tf_op jit(solution)/shard_map/ppermute | solution.py:226
  26.6 8.7 %collective-permute-start.81 = (bf16[192,512]{1,0:T(8,128)(2,1)}, bf16[192,512]{1,0:T(8,128)(2,1)S(1)}, u32[]{:S(2)}, u32[]{:S(2)}) collective-permute-start(bf16[192,512]{1,0:T(8,128)(2,1)} %get-tuple-element.359), channel_id=1, source_target_pairs={{0,2},{1,3},{2,0},{3,1},{4,6},{5,7},{6,4},{7,5},{8,10},{9,11},{10,... | collective-permute-start | bytes 589832 | tf_op jit(solution)/shard_map/ppermute | solution.py:226
  29.4 14.0 %collective-permute-start.82 = (bf16[192,512]{1,0:T(8,128)(2,1)}, bf16[192,512]{1,0:T(8,128)(2,1)S(1)}, u32[]{:S(2)}, u32[]{:S(2)}) collective-permute-start(bf16[192,512]{1,0:T(8,128)(2,1)} %get-tuple-element.360), channel_id=1, source_target_pairs={{0,3},{1,2},{2,1},{3,0},{4,7},{5,6},{6,5},{7,4},{8,11},{9,10},{10,... | collective-permute-start | bytes 589832 | tf_op jit(solution)/shard_map/ppermute | solution.py:226
  29.5 13.9 %collective-permute-start.83 = (bf16[192,512]{1,0:T(8,128)(2,1)}, bf16[192,512]{1,0:T(8,128)(2,1)S(1)}, u32[]{:S(2)}, u32[]{:S(2)}) collective-permute-start(bf16[192,512]{1,0:T(8,128)(2,1)} %get-tuple-element.361), channel_id=1, source_target_pairs={{0,4},{1,5},{2,6},{3,7},{4,0},{5,1},{6,2},{7,3},{8,12},{9,13},{10,... | collective-permute-start | bytes 589832 | tf_op jit(solution)/shard_map/ppermute | solution.py:226
  30.8 17.6 %collective-permute-start.84 = (bf16[192,512]{1,0:T(8,128)(2,1)}, bf16[192,512]{1,0:T(8,128)(2,1)S(1)}, u32[]{:S(2)}, u32[]{:S(2)}) collective-permute-start(bf16[192,512]{1,0:T(8,128)(2,1)} %get-tuple-element.362), channel_id=1, source_target_pairs={{0,5},{1,4},{2,7},{3,6},{4,1},{5,0},{6,3},{7,2},{8,13},{9,12},{10,... | collective-permute-start | bytes 589832 | tf_op jit(solution)/shard_map/ppermute | solution.py:226
  30.9 17.5 %collective-permute-start.85 = (bf16[192,512]{1,0:T(8,128)(2,1)}, bf16[192,512]{1,0:T(8,128)(2,1)S(1)}, u32[]{:S(2)}, u32[]{:S(2)}) collective-permute-start(bf16[192,512]{1,0:T(8,128)(2,1)} %get-tuple-element.363), channel_id=1, source_target_pairs={{0,6},{1,7},{2,4},{3,5},{4,2},{5,3},{6,0},{7,1},{8,14},{9,15},{10,... | collective-permute-start | bytes 589832 | tf_op jit(solution)/shard_map/ppermute | solution.py:226
  35.3 13.0 %collective-permute-start.86 = (bf16[192,512]{1,0:T(8,128)(2,1)}, bf16[192,512]{1,0:T(8,128)(2,1)S(1)}, u32[]{:S(2)}, u32[]{:S(2)}) collective-permute-start(bf16[192,512]{1,0:T(8,128)(2,1)} %get-tuple-element.364), channel_id=1, source_target_pairs={{0,7},{1,6},{2,5},{3,4},{4,3},{5,2},{6,1},{7,0},{8,15},{9,14},{10,... | collective-permute-start | bytes 589832 | tf_op jit(solution)/shard_map/ppermute | solution.py:226
  48.4 4.2 %collective-permute-start.35 = (bf16[192,512]{1,0:T(8,128)(2,1)}, bf16[192,512]{1,0:T(8,128)(2,1)S(1)}, u32[]{:S(2)}, u32[]{:S(2)}) collective-permute-start(bf16[192,512]{1,0:T(8,128)(2,1)} %get-tuple-element.291), channel_id=1, source_target_pairs={{0,1},{1,0},{2,3},{3,2},{4,5},{5,4},{6,7},{7,6},{8,9},{9,8},{10,11... | collective-permute-start | bytes 589832 | tf_op jit(solution)/shard_map/cond/branch_1_fun/ppermute | solution.py:226
  49.1 8.0 %collective-permute-start.36 = (bf16[192,512]{1,0:T(8,128)(2,1)}, bf16[192,512]{1,0:T(8,128)(2,1)S(1)}, u32[]{:S(2)}, u32[]{:S(2)}) collective-permute-start(bf16[192,512]{1,0:T(8,128)(2,1)} %get-tuple-element.292), channel_id=1, source_target_pairs={{0,2},{1,3},{2,0},{3,1},{4,6},{5,7},{6,4},{7,5},{8,10},{9,11},{10,... | collective-permute-start | bytes 589832 | tf_op jit(solution)/shard_map/cond/branch_1_fun/ppermute | solution.py:226
  51.0 9.8 %collective-permute-start.37 = (bf16[192,512]{1,0:T(8,128)(2,1)}, bf16[192,512]{1,0:T(8,128)(2,1)S(1)}, u32[]{:S(2)}, u32[]{:S(2)}) collective-permute-start(bf16[192,512]{1,0:T(8,128)(2,1)} %get-tuple-element.293), channel_id=1, source_target_pairs={{0,3},{1,2},{2,1},{3,0},{4,7},{5,6},{6,5},{7,4},{8,11},{9,10},{10,... | collective-permute-start | bytes 589832 | tf_op jit(solution)/shard_map/cond/branch_1_fun/ppermute | solution.py:226
  51.0 11.1 %collective-permute-start.38 = (bf16[192,512]{1,0:T(8,128)(2,1)}, bf16[192,512]{1,0:T(8,128)(2,1)S(1)}, u32[]{:S(2)}, u32[]{:S(2)}) collective-permute-start(bf16[192,512]{1,0:T(8,128)(2,1)} %get-tuple-element.294), channel_id=1, source_target_pairs={{0,4},{1,5},{2,6},{3,7},{4,0},{5,1},{6,2},{7,3},{8,12},{9,13},{10,... | collective-permute-start | bytes 589832 | tf_op jit(solution)/shard_map/cond/branch_1_fun/ppermute | solution.py:226
  52.0 18.1 %collective-permute-start.39 = (bf16[192,512]{1,0:T(8,128)(2,1)}, bf16[192,512]{1,0:T(8,128)(2,1)S(1)}, u32[]{:S(2)}, u32[]{:S(2)}) collective-permute-start(bf16[192,512]{1,0:T(8,128)(2,1)} %get-tuple-element.295), channel_id=1, source_target_pairs={{0,5},{1,4},{2,7},{3,6},{4,1},{5,0},{6,3},{7,2},{8,13},{9,12},{10,... | collective-permute-start | bytes 589832 | tf_op jit(solution)/shard_map/cond/branch_1_fun/ppermute | solution.py:226
  52.6 17.5 %collective-permute-start.40 = (bf16[192,512]{1,0:T(8,128)(2,1)}, bf16[192,512]{1,0:T(8,128)(2,1)S(1)}, u32[]{:S(2)}, u32[]{:S(2)}) collective-permute-start(bf16[192,512]{1,0:T(8,128)(2,1)} %get-tuple-element.296), channel_id=1, source_target_pairs={{0,6},{1,7},{2,4},{3,5},{4,2},{5,3},{6,0},{7,1},{8,14},{9,15},{10,... | collective-permute-start | bytes 589832 | tf_op jit(solution)/shard_map/cond/branch_1_fun/ppermute | solution.py:226
  57.0 13.0 %collective-permute-start.41 = (bf16[192,512]{1,0:T(8,128)(2,1)}, bf16[192,512]{1,0:T(8,128)(2,1)S(1)}, u32[]{:S(2)}, u32[]{:S(2)}) collective-permute-start(bf16[192,512]{1,0:T(8,128)(2,1)} %get-tuple-element.297), channel_id=1, source_target_pairs={{0,7},{1,6},{2,5},{3,4},{4,3},{5,2},{6,1},{7,0},{8,15},{9,14},{10,... | collective-permute-start | bytes 589832 | tf_op jit(solution)/shard_map/cond/branch_1_fun/ppermute | solution.py:226
  60.8 28.1 %collective-permute-start.25 = (bf16[1024,512]{1,0:T(8,128)(2,1)}, bf16[1024,512]{1,0:T(8,128)(2,1)}, u32[]{:S(2)}, u32[]{:S(2)}) collective-permute-start(bf16[1024,512]{1,0:T(8,128)(2,1)} %window.8), channel_id=1, source_target_pairs={{8,0},{9,1},{10,2},{11,3},{12,4},{13,5},{14,6},{15,7},{16,8},{17,9... | collective-permute-start | bytes 3145736 | tf_op jit(solution)/shard_map/cond/branch_1_fun/ppermute | solution.py:277
  74.2 37.1 %collective-permute-start.42 = (bf16[1024,512]{1,0:T(8,128)(2,1)}, bf16[1024,512]{1,0:T(8,128)(2,1)S(1)}, u32[]{:S(2)}, u32[]{:S(2)}) collective-permute-start(bf16[1024,512]{1,0:T(8,128)(2,1)} %window.9), channel_id=1, source_target_pairs={{8,0},{9,1},{10,2},{11,3},{12,4},{13,5},{14,6},{15,7},{16,8},{17,9... | collective-permute-start | bytes 3145736 | tf_op jit(solution)/shard_map/cond/branch_1_fun/ppermute | solution.py:277
  88.9 44.8 %collective-permute-start.26 = (bf16[1024,512]{1,0:T(8,128)(2,1)}, bf16[1024,512]{1,0:T(8,128)(2,1)S(1)}, u32[]{:S(2)}, u32[]{:S(2)}) collective-permute-start(bf16[1024,512]{1,0:T(8,128)(2,1)} %collective-permute-done.25.rest_8_), channel_id=1, source_target_pairs={{8,0},{9,1},{10,2},{11,3},{12,4},{13,5},{14,6},{15,7},{16,8},{17,9... | collective-permute-start | bytes 3145736 | tf_op jit(solution)/shard_map/cond/branch_1_fun/ppermute | solution.py:277
  111.3 45.7 %copy-start.8 = (bf16[1024,512]{1,0:T(8,128)(2,1)}, bf16[1024,512]{1,0:T(8,128)(2,1)S(1)}, u32[]{:S(2)}) copy-start(bf16[1024,512]{1,0:T(8,128)(2,1)S(1)} %collective-permute-done.42.rest_8_) | copy-start | bytes 3145732 | tf_op jit(solution)/shard_map/cond
  111.3 44.9 %collective-permute-start.43 = (bf16[1024,512]{1,0:T(8,128)(2,1)S(1)}, bf16[1024,512]{1,0:T(8,128)(2,1)S(1)}, u32[]{:S(2)}, u32[]{:S(2)}) collective-permute-start(bf16[1024,512]{1,0:T(8,128)(2,1)S(1)} %collective-permute-done.42.rest_8_), channel_id=1, source_target_pairs={{8,0},{9,1},{10,2},{11,3},{12,4},{13,5},{14,6},{15,7},{16,8},{17,9... | collective-permute-start | bytes 3145736 | tf_op jit(solution)/shard_map/cond/branch_1_fun/ppermute | solution.py:277
  133.7 22.5 %copy-start.7 = (bf16[1024,512]{1,0:T(8,128)(2,1)}, bf16[1024,512]{1,0:T(8,128)(2,1)S(1)}, u32[]{:S(2)}) copy-start(bf16[1024,512]{1,0:T(8,128)(2,1)S(1)} %collective-permute-done.26.rest_9_) | copy-start | bytes 3145732 | tf_op jit(solution)/shard_map/cond
  133.8 28.1 %collective-permute-start.27 = (bf16[256,512]{1,0:T(8,128)(2,1)S(1)}, bf16[256,512]{1,0:T(8,128)(2,1)S(1)}, u32[]{:S(2)}, u32[]{:S(2)}) collective-permute-start(bf16[256,512]{1,0:T(8,128)(2,1)S(1)} %slice.14), channel_id=1, source_target_pairs={{8,0},{9,1},{10,2},{11,3},{12,4},{13,5},{14,6},{15,7},{16,8},{17,9... | collective-permute-start | bytes 786440 | tf_op jit(solution)/shard_map/cond/branch_1_fun/ppermute | solution.py:277
  157.0 13.2 %collective-permute-start.44 = (bf16[256,512]{1,0:T(8,128)(2,1)}, bf16[256,512]{1,0:T(8,128)(2,1)S(1)}, u32[]{:S(2)}, u32[]{:S(2)}) collective-permute-start(bf16[256,512]{1,0:T(8,128)(2,1)} %slice.15), channel_id=1, source_target_pairs={{8,0},{9,1},{10,2},{11,3},{12,4},{13,5},{14,6},{15,7},{16,8},{17,9... | collective-permute-start | bytes 786440 | tf_op jit(solution)/shard_map/cond/branch_1_fun/ppermute | solution.py:277
  167.5 9.3 %collective-permute-start.28 = (bf16[192,512]{1,0:T(8,128)(2,1)}, bf16[192,512]{1,0:T(8,128)(2,1)S(1)}, u32[]{:S(2)}, u32[]{:S(2)}) collective-permute-start(bf16[192,512]{1,0:T(8,128)(2,1)} %get-tuple-element.283), channel_id=1, source_target_pairs={{0,1},{1,0},{2,3},{3,2},{4,5},{5,4},{6,7},{7,6},{8,9},{9,8},{10,11... | collective-permute-start | bytes 589832 | tf_op jit(solution)/shard_map/cond/branch_1_fun/ppermute | solution.py:226
  167.7 10.1 %collective-permute-start.29 = (bf16[192,512]{1,0:T(8,128)(2,1)}, bf16[192,512]{1,0:T(8,128)(2,1)S(1)}, u32[]{:S(2)}, u32[]{:S(2)}) collective-permute-start(bf16[192,512]{1,0:T(8,128)(2,1)} %get-tuple-element.284), channel_id=1, source_target_pairs={{0,2},{1,3},{2,0},{3,1},{4,6},{5,7},{6,4},{7,5},{8,10},{9,11},{10,... | collective-permute-start | bytes 589832 | tf_op jit(solution)/shard_map/cond/branch_1_fun/ppermute | solution.py:226
  168.6 11.1 %collective-permute-start.30 = (bf16[192,512]{1,0:T(8,128)(2,1)}, bf16[192,512]{1,0:T(8,128)(2,1)S(1)}, u32[]{:S(2)}, u32[]{:S(2)}) collective-permute-start(bf16[192,512]{1,0:T(8,128)(2,1)} %get-tuple-element.285), channel_id=1, source_target_pairs={{0,3},{1,2},{2,1},{3,0},{4,7},{5,6},{6,5},{7,4},{8,11},{9,10},{10,... | collective-permute-start | bytes 589832 | tf_op jit(solution)/shard_map/cond/branch_1_fun/ppermute | solution.py:226
  169.4 10.6 %collective-permute-start.31 = (bf16[192,512]{1,0:T(8,128)(2,1)}, bf16[192,512]{1,0:T(8,128)(2,1)S(1)}, u32[]{:S(2)}, u32[]{:S(2)}) collective-permute-start(bf16[192,512]{1,0:T(8,128)(2,1)} %get-tuple-element.286), channel_id=1, source_target_pairs={{0,4},{1,5},{2,6},{3,7},{4,0},{5,1},{6,2},{7,3},{8,12},{9,13},{10,... | collective-permute-start | bytes 589832 | tf_op jit(solution)/shard_map/cond/branch_1_fun/ppermute | solution.py:226
  170.2 10.8 %collective-permute-start.32 = (bf16[192,512]{1,0:T(8,128)(2,1)}, bf16[192,512]{1,0:T(8,128)(2,1)S(1)}, u32[]{:S(2)}, u32[]{:S(2)}) collective-permute-start(bf16[192,512]{1,0:T(8,128)(2,1)} %get-tuple-element.287), channel_id=1, source_target_pairs={{0,5},{1,4},{2,7},{3,6},{4,1},{5,0},{6,3},{7,2},{8,13},{9,12},{10,... | collective-permute-start | bytes 589832 | tf_op jit(solution)/shard_map/cond/branch_1_fun/ppermute | solution.py:226
  176.9 31.3 %copy-start.29 = (bf16[192,512]{1,0:T(8,128)(2,1)}, bf16[192,512]{1,0:T(8,128)(2,1)S(1)}, u32[]{:S(2)}) copy-start(bf16[192,512]{1,0:T(8,128)(2,1)S(1)} %collective-permute-done.28.rest_1_) | copy-start | bytes 589828 | tf_op jit(solution)/shard_map/cond
  176.9 12.8 %collective-permute-start.33 = (bf16[192,512]{1,0:T(8,128)(2,1)S(1)}, bf16[192,512]{1,0:T(8,128)(2,1)S(1)}, u32[]{:S(2)}, u32[]{:S(2)}) collective-permute-start(bf16[192,512]{1,0:T(8,128)(2,1)S(1)} %copy-done.70), channel_id=1, source_target_pairs={{0,6},{1,7},{2,4},{3,5},{4,2},{5,3},{6,0},{7,1},{8,14},{9,15},{10,... | collective-permute-start | bytes 589832 | tf_op jit(solution)/shard_map/cond/branch_1_fun/ppermute | solution.py:226
  177.9 30.4 %copy-start.31 = (bf16[192,512]{1,0:T(8,128)(2,1)}, bf16[192,512]{1,0:T(8,128)(2,1)S(1)}, u32[]{:S(2)}) copy-start(bf16[192,512]{1,0:T(8,128)(2,1)S(1)} %collective-permute-done.29.rest_2_) | copy-start | bytes 589828 | tf_op jit(solution)/shard_map/cond
  177.9 12.2 %collective-permute-start.34 = (bf16[192,512]{1,0:T(8,128)(2,1)S(1)}, bf16[192,512]{1,0:T(8,128)(2,1)S(1)}, u32[]{:S(2)}, u32[]{:S(2)}) collective-permute-start(bf16[192,512]{1,0:T(8,128)(2,1)S(1)} %copy-done.68), channel_id=1, source_target_pairs={{0,7},{1,6},{2,5},{3,4},{4,3},{5,2},{6,1},{7,0},{8,15},{9,14},{10,... | collective-permute-start | bytes 589832 | tf_op jit(solution)/shard_map/cond/branch_1_fun/ppermute | solution.py:226
  179.7 28.6 %copy-start.33 = (bf16[192,512]{1,0:T(8,128)(2,1)}, bf16[192,512]{1,0:T(8,128)(2,1)S(1)}, u32[]{:S(2)}) copy-start(bf16[192,512]{1,0:T(8,128)(2,1)S(1)} %collective-permute-done.30.rest_3_) | copy-start | bytes 589828 | tf_op jit(solution)/shard_map/cond
  179.7 11.3 %collective-permute-start.45 = (bf16[192,512]{1,0:T(8,128)(2,1)}, bf16[192,512]{1,0:T(8,128)(2,1)S(1)}, u32[]{:S(2)}, u32[]{:S(2)}) collective-permute-start(bf16[192,512]{1,0:T(8,128)(2,1)} %get-tuple-element.299), channel_id=1, source_target_pairs={{0,1},{1,0},{2,3},{3,2},{4,5},{5,4},{6,7},{7,6},{8,9},{9,8},{10,11... | collective-permute-start | bytes 589832 | tf_op jit(solution)/shard_map/cond/branch_1_fun/ppermute | solution.py:226
  180.1 28.2 %copy-start.35 = (bf16[192,512]{1,0:T(8,128)(2,1)}, bf16[192,512]{1,0:T(8,128)(2,1)S(1)}, u32[]{:S(2)}) copy-start(bf16[192,512]{1,0:T(8,128)(2,1)S(1)} %collective-permute-done.31.rest_4_) | copy-start | bytes 589828 | tf_op jit(solution)/shard_map/cond
  180.1 13.4 %collective-permute-start.46 = (bf16[192,512]{1,0:T(8,128)(2,1)}, bf16[192,512]{1,0:T(8,128)(2,1)S(1)}, u32[]{:S(2)}, u32[]{:S(2)}) collective-permute-start(bf16[192,512]{1,0:T(8,128)(2,1)} %get-tuple-element.300), channel_id=1, source_target_pairs={{0,2},{1,3},{2,0},{3,1},{4,6},{5,7},{6,4},{7,5},{8,10},{9,11},{10,... | collective-permute-start | bytes 589832 | tf_op jit(solution)/shard_map/cond/branch_1_fun/ppermute | solution.py:226
  181.0 27.3 %copy-start.37 = (bf16[192,512]{1,0:T(8,128)(2,1)}, bf16[192,512]{1,0:T(8,128)(2,1)S(1)}, u32[]{:S(2)}) copy-start(bf16[192,512]{1,0:T(8,128)(2,1)S(1)} %collective-permute-done.32.rest_5_) | copy-start | bytes 589828 | tf_op jit(solution)/shard_map/cond
  181.0 15.3 %collective-permute-start.47 = (bf16[192,512]{1,0:T(8,128)(2,1)}, bf16[192,512]{1,0:T(8,128)(2,1)S(1)}, u32[]{:S(2)}, u32[]{:S(2)}) collective-permute-start(bf16[192,512]{1,0:T(8,128)(2,1)} %get-tuple-element.301), channel_id=1, source_target_pairs={{0,3},{1,2},{2,1},{3,0},{4,7},{5,6},{6,5},{7,4},{8,11},{9,10},{10,... | collective-permute-start | bytes 589832 | tf_op jit(solution)/shard_map/cond/branch_1_fun/ppermute | solution.py:226
  189.7 18.5 %copy-start.41 = (bf16[192,512]{1,0:T(8,128)(2,1)}, bf16[192,512]{1,0:T(8,128)(2,1)S(1)}, u32[]{:S(2)}) copy-start(bf16[192,512]{1,0:T(8,128)(2,1)S(1)} %collective-permute-done.33.rest_6_) | copy-start | bytes 589828 | tf_op jit(solution)/shard_map/cond
  189.7 8.5 %collective-permute-start.48 = (bf16[192,512]{1,0:T(8,128)(2,1)}, bf16[192,512]{1,0:T(8,128)(2,1)S(1)}, u32[]{:S(2)}, u32[]{:S(2)}) collective-permute-start(bf16[192,512]{1,0:T(8,128)(2,1)} %get-tuple-element.302), channel_id=1, source_target_pairs={{0,4},{1,5},{2,6},{3,7},{4,0},{5,1},{6,2},{7,3},{8,12},{9,13},{10,... | collective-permute-start | bytes 589832 | tf_op jit(solution)/shard_map/cond/branch_1_fun/ppermute | solution.py:226
  190.0 18.2 %copy-start.44 = (bf16[192,512]{1,0:T(8,128)(2,1)}, bf16[192,512]{1,0:T(8,128)(2,1)S(1)}, u32[]{:S(2)}) copy-start(bf16[192,512]{1,0:T(8,128)(2,1)S(1)} %collective-permute-done.34.rest_7_) | copy-start | bytes 589828 | tf_op jit(solution)/shard_map/cond
  190.0 18.1 %collective-permute-start.49 = (bf16[192,512]{1,0:T(8,128)(2,1)}, bf16[192,512]{1,0:T(8,128)(2,1)S(1)}, u32[]{:S(2)}, u32[]{:S(2)}) collective-permute-start(bf16[192,512]{1,0:T(8,128)(2,1)} %get-tuple-element.303), channel_id=1, source_target_pairs={{0,5},{1,4},{2,7},{3,6},{4,1},{5,0},{6,3},{7,2},{8,13},{9,12},{10,... | collective-permute-start | bytes 589832 | tf_op jit(solution)/shard_map/cond/branch_1_fun/ppermute | solution.py:226
  191.0 17.2 %collective-permute-start.50 = (bf16[192,512]{1,0:T(8,128)(2,1)}, bf16[192,512]{1,0:T(8,128)(2,1)S(1)}, u32[]{:S(2)}, u32[]{:S(2)}) collective-permute-start(bf16[192,512]{1,0:T(8,128)(2,1)} %get-tuple-element.304), channel_id=1, source_target_pairs={{0,6},{1,7},{2,4},{3,5},{4,2},{5,3},{6,0},{7,1},{8,14},{9,15},{10,... | collective-permute-start | bytes 589832 | tf_op jit(solution)/shard_map/cond/branch_1_fun/ppermute | solution.py:226
  193.5 14.7 %collective-permute-start.51 = (bf16[192,512]{1,0:T(8,128)(2,1)}, bf16[192,512]{1,0:T(8,128)(2,1)S(1)}, u32[]{:S(2)}, u32[]{:S(2)}) collective-permute-start(bf16[192,512]{1,0:T(8,128)(2,1)} %get-tuple-element.305), channel_id=1, source_target_pairs={{0,7},{1,6},{2,5},{3,4},{4,3},{5,2},{6,1},{7,0},{8,15},{9,14},{10,... | collective-permute-start | bytes 589832 | tf_op jit(solution)/shard_map/cond/branch_1_fun/ppermute | solution.py:226
  (20 other events, 135.0 us)
